TPU v7x, 32 devices: a whole 2x2x4 slice. The times are simulated.
32 devices in a mesh: tp: 8 (over z, y), kv: 4 (over x, core).
Axes of the slice: x: 2, y: 2, z: 4, core: 2. Of those that a mesh axis runs over, the one named last changes fastest.
Arguments:
- hidden_in: bfloat16 [2048, 4096], P(('kv', 'tp')), may hold values from -6 to 6
- gain_attn: float32 [4096], replicated, may hold values from 0.4 to 1.6
- w_qkv: bfloat16 [4096, 32, 384], P(None, 'tp'), may hold values from -0.09375 to 0.09375
- cache_kv: bfloat16 [2, 8192, 32, 256], P(None, 'kv', 'tp'), may hold values from -110 to 110
- cache_len: int32 [2], replicated, may hold values from 128 to 8192, as said below
- w_out: bfloat16 [4096, 4096], P('tp'), may hold values from -0.1875 to 0.1875
- gain_mlp: float32 [4096], replicated, may hold values from 0.1 to 1.9
- w_gate_up: bfloat16 [4096, 2, 11008], P('kv', None, 'tp'), may hold values from -0.09375 to 0.09375
- w_down: bfloat16 [11008, 4096], P('tp', 'kv'), may hold values from -0.0546875 to 0.0546875
Outputs:
- layer_out: bfloat16 [2048, 4096], P(('kv', 'tp'))
Inputs may be any that keep to these rules, and one draw needn't show every extreme that they name: `cache_len`: every length is a multiple of 128; some sequence uses the whole cache.
All inputs are finite; a program needn't handle non-finite values.
Results may differ from a plain program's by a relative error of at most 0.019.
The roundings to bfloat16 on the way count: a program that leaves them out, or rounds other values in their place, can miss the bound.
Values may be sent and summed in bfloat16 or wider, within the bound.
A program may use at most 192 MiB of HBM per device.

v0:
```python
import math
import jax
import jax.numpy as jnp
from jax import lax
from jax.sharding import PartitionSpec as P

EPSILON = 1e-05
MASKED = -1e30


def rms_scale(values_in, gain_vector):
    widened = values_in.astype(jnp.float32)
    mean_square = jnp.mean(widened * widened, axis=-1, keepdims=True)
    return (widened * lax.rsqrt(mean_square + EPSILON) * gain_vector).astype(jnp.bfloat16)


def per_device(
    hidden_in, gain_attn, w_qkv, cache_kv, cache_len, w_out, gain_mlp, w_gate_up, w_down
):
    local_heads = w_qkv.shape[1]
    head_dim = w_qkv.shape[2] // 3
    own_rows = hidden_in.shape[0]
    block_input = lax.all_gather(hidden_in, "tp", axis=0, tiled=True)
    block_rows = block_input.shape[0]
    normed = rms_scale(block_input, gain_attn)
    flat_qkv = w_qkv.reshape(w_qkv.shape[0], local_heads * 3 * head_dim)
    packed = jnp.dot(normed, flat_qkv, preferred_element_type=jnp.float32).astype(jnp.bfloat16)
    packed = packed.reshape(block_rows, local_heads, 3 * head_dim)
    key_mine = packed[:, :, head_dim : 2 * head_dim]
    value_mine = packed[:, :, 2 * head_dim :]
    query_rows = lax.all_gather(packed[:, :, :head_dim], "kv", axis=0, tiled=True)
    seq_count = cache_kv.shape[0]
    span_len = query_rows.shape[0] // seq_count
    kv_index = lax.axis_index("kv")
    cache_rows = cache_kv.shape[1]
    cache_pos = kv_index * cache_rows + jnp.arange(cache_rows, dtype=jnp.int32)
    own_seq = (kv_index * block_rows + jnp.arange(block_rows, dtype=jnp.int32)) // span_len
    row_peaks, masses, accums = ([], [], [])
    for seq_id in range(seq_count):
        query_block = query_rows[seq_id * span_len : (seq_id + 1) * span_len]
        joined_key_rows = jnp.concatenate([cache_kv[seq_id, :, :, :head_dim], key_mine], axis=0)
        joined_value_rows = jnp.concatenate([cache_kv[seq_id, :, :, head_dim:], value_mine], axis=0)
        usable = jnp.concatenate([cache_pos < cache_len[seq_id], own_seq == seq_id])
        logit_scores = jnp.einsum(
            "qhd,khd->hqk", query_block, joined_key_rows, preferred_element_type=jnp.float32
        ) / math.sqrt(head_dim)
        logit_scores = jnp.where(usable[None, None, :], logit_scores, MASKED)
        row_peak = jnp.max(logit_scores, axis=2)
        raw_weights = jnp.where(
            usable[None, None, :], jnp.exp(logit_scores - row_peak[:, :, None]), 0.0
        )
        row_peaks.append(row_peak.T)
        masses.append(jnp.sum(raw_weights, axis=2).T)
        accums.append(
            jnp.einsum(
                "hqk,khd->qhd",
                raw_weights.astype(jnp.bfloat16),
                joined_value_rows,
                preferred_element_type=jnp.float32,
            )
        )
    peak_all = jnp.concatenate(row_peaks, axis=0)
    mass_all = jnp.concatenate(masses, axis=0)
    accum_all = jnp.concatenate(accums, axis=0)
    peak_set, mass_set, accum_set = (
        lax.all_to_all(peak_all[None], "kv", split_axis=1, concat_axis=0, tiled=True),
        lax.all_to_all(mass_all[None], "kv", split_axis=1, concat_axis=0, tiled=True),
        lax.all_to_all(accum_all[None], "kv", split_axis=1, concat_axis=0, tiled=True),
    )
    peak_best = jnp.max(peak_set, axis=0)
    scaling = jnp.exp(peak_set - peak_best[None])
    mass_own = jnp.sum(mass_set * scaling, axis=0)
    accum_own = jnp.sum(accum_set * scaling[..., None], axis=0)
    attended = (
        (accum_own / mass_own[..., None])
        .astype(jnp.bfloat16)
        .reshape(block_rows, local_heads * head_dim)
    )
    tp_index = lax.axis_index("tp")
    heads_sum = lax.psum(
        jnp.dot(attended, w_out, preferred_element_type=jnp.float32).astype(jnp.bfloat16), "tp"
    ).astype(jnp.float32)
    residual = block_input.astype(jnp.float32) + heads_sum
    mlp_in = rms_scale(residual, gain_mlp)
    residual_own = lax.dynamic_slice_in_dim(residual, tp_index * own_rows, own_rows, 0)
    gate_up = jnp.einsum(
        "td,dgf->tgf",
        mlp_in,
        lax.all_gather(w_gate_up, "kv", axis=0, tiled=True),
        preferred_element_type=jnp.float32,
    )
    activated = (jax.nn.silu(gate_up[:, 0, :]) * gate_up[:, 1, :]).astype(jnp.bfloat16)
    down_terms = jnp.dot(
        activated,
        lax.all_gather(w_down, "kv", axis=1, tiled=True),
        preferred_element_type=jnp.float32,
    )
    down_own = lax.psum_scatter(
        down_terms.astype(jnp.bfloat16), "tp", scatter_dimension=0, tiled=True
    ).astype(jnp.float32)
    return (residual_own + down_own).astype(jnp.bfloat16)


def solution(mesh):
    in_specs = (
        P(("kv", "tp"), None),
        P(),
        P(None, "tp", None),
        P(None, "kv", "tp", None),
        P(),
        P("tp", None),
        P(),
        P("kv", None, "tp"),
        P("tp", "kv"),
    )
    out_specs = P(("kv", "tp"), None)
    return jax.shard_map(
        per_device, mesh=mesh, in_specs=in_specs, out_specs=out_specs, check_vma=False
    )
```

profile of v0, /device:TPU:0, one launch (start us, length us, event | category | flops | bytes accessed | tf_op | source)
XLA Modules:
  0.0 827.3 jit_solution(16002876231132787441)
XLA Ops:
  7.3 12.4 %copy.51 = bf16[512,8,4,384]{3,1,2,0:T(8,128)(2,1)} copy(bf16[512,8,4,384]{3,2,1,0:T(4,128)(2,1)} %bitcast.50) | data formatting | bytes 25165824
  19.7 65.3 %all-gather.5.cloned.1.call-done = bf16[512,4096]{1,0:T(8,128)(2,1)} async-done(((bf16[64,4096]{1,0:T(8,128)(2,1)}), bf16[512,4096]{1,0:T(8,128)(2,1)}) %all-gather.5.cloned.1.call-update) | async-done | bytes 4194320 | tf_op jit(solution)/shard_map/all_gather | solution.py:23
  88.1 11.0 %fusion.24 = bf16[512,1536]{1,0:T(8,128)(2,1)S(1)} fusion(bf16[4096,1536]{1,0:T(8,128)(2,1)} %bitcast.51, bf16[512,4096]{1,0:T(8,128)(2,1)} %all-gather.5.cloned.1.call-done, f32[4096]{0:T(1024)S(1)} %copy-done.5, f32[512]{0:T(512)S(1)} %add_rsqrt_fusion.1), kind=kOutput, calls=%fused_computation.37 | convolution fusion | flops 6451625984 | bytes 18368512 | tf_op jit(solution)/shard_map/dot_general | solution.py:27
  100.9 6.4 fusion.61
  122.2 19.7 %fusion.1 = (f32[4,1024]{1,0:T(4,128)S(1)}, f32[4,1024,2560]{2,1,0:T(8,128)}) fusion(pred[2560]{0:T(1024)(128)(4,1)S(1)} %pad_add_fusion.1, bf16[512,4,128]{2,0,1:T(8,128)(2,1)S(1)} %copy.48, bf16[2048,4,128]{2,0,1:T(8,128)(2,1)} %get-tuple-element.26, bf16[2048,4,128]{2,0,1:T(8,128)(2,1)} %all-gather.7.cloned.1.call-done), kind=kOutput, calls=%fused_computation.5 | convolution fusion | flops 2721050624 | bytes 45632000 | tf_op jit(solution)/shard_map/qhd,khd->hqk/dot_general | solution.py:44
  141.8 19.2 %fusion.4 = f32[4,1024]{1,0:T(4,128)S(1)} fusion(f32[4,1024,2560]{2,1,0:T(8,128)} %get-tuple-element.19, f32[4,1024]{1,0:T(4,128)S(1)} %get-tuple-element.18, pred[2560]{0:T(1024)(128)(4,1)S(1)} %pad_add_fusion.1), kind=kLoop, calls=%fused_computation.8 | loop fusion | flops 52424704 | bytes 41978368 | tf_op jit(solution)/shard_map/reduce_sum | solution.py:53
  161.1 17.9 %fusion.38 = f32[1024,4,128]{0,2,1:T(8,128)} fusion(f32[4,1024,2560]{2,1,0:T(8,128)} %get-tuple-element.19, f32[4,1024]{1,0:T(4,128)S(1)} %get-tuple-element.18, pred[2560]{0:T(1024)(128)(4,1)S(1)} %pad_add_fusion.1, bf16[512,4,128]{0,2,1:T(8,128)(2,1)S(1)} %copy-done.3, bf16[2048,4,128]{0,2,1:T(8,128)(2,1)S(1)} %bitcast.59), kind=kOutput, calls=%fused_computation.51 | convolution fusion | flops 2742026240 | bytes 46680576 | tf_op jit(solution)/shard_map/hqk,khd->qhd/dot_general | solution.py:55
  178.9 19.0 %fusion = (f32[4,1024]{1,0:T(4,128)S(1)}, f32[4,1024,2560]{2,1,0:T(8,128)}) fusion(pred[2560]{0:T(1024)(128)(4,1)S(1)} %pad_add_fusion, bf16[512,4,128]{2,0,1:T(8,128)(2,1)S(1)} %copy.48, bf16[2048,4,128]{2,0,1:T(8,128)(2,1)S(1)} %get-tuple-element.27, bf16[2048,4,128]{2,0,1:T(8,128)(2,1)} %all-gather.7.cloned.1.call-done), kind=kOutput, calls=%fused_computation.4 | convolution fusion | flops 2721050624 | bytes 45632000 | tf_op jit(solution)/shard_map/qhd,khd->hqk/dot_general | solution.py:44
  198.0 19.2 %fusion.2 = f32[4,1024]{1,0:T(4,128)S(1)} fusion(f32[4,1024,2560]{2,1,0:T(8,128)} %get-tuple-element.21, f32[4,1024]{1,0:T(4,128)S(1)} %get-tuple-element.20, pred[2560]{0:T(1024)(128)(4,1)S(1)} %pad_add_fusion), kind=kLoop, calls=%fused_computation.6 | loop fusion | flops 52424704 | bytes 41978368 | tf_op jit(solution)/shard_map/reduce_sum | solution.py:53
  217.2 17.9 %fusion.35 = f32[1024,4,128]{0,2,1:T(8,128)} fusion(f32[4,1024,2560]{2,1,0:T(8,128)} %get-tuple-element.21, f32[4,1024]{1,0:T(4,128)S(1)} %get-tuple-element.20, pred[2560]{0:T(1024)(128)(4,1)S(1)} %pad_add_fusion, bf16[512,4,128]{0,2,1:T(8,128)(2,1)S(1)} %copy-done.3, bf16[2048,4,128]{0,2,1:T(8,128)(2,1)S(1)} %bitcast.58), kind=kOutput, calls=%fused_computation.50 | convolution fusion | flops 2742026240 | bytes 46680576 | tf_op jit(solution)/shard_map/hqk,khd->qhd/dot_general | solution.py:55
  236.1 9.5 %reduce.2 = f32[2048,4]{1,0:T(8,128)S(1)} reduce(f32[2048,1,4]{2,1,0:T(1,128)S(1)} %bitcast.54, f32[]{:T(128)} %broadcast.98), dimensions={1}, to_apply=%bitcast.41.reduce_sub_computation | reduce | bytes 65540
  250.6 9.3 %reduce = f32[2048,4]{1,0:T(8,128)S(1)} reduce(f32[2048,1,4]{2,1,0:T(1,128)S(1)} %bitcast.55, f32[]{:T(128)} %broadcast.98), dimensions={1}, to_apply=%bitcast.43.reduce_sub_computation | reduce | bytes 65540
  269.2 5.2 copy.37
  274.5 4.9 all-to-all-start
  285.5 42.0 %all-to-all-done = f32[1,2048,4,128]{3,2,0,1:T(4,128)} async-done(((f32[1,2048,4,128]{3,2,0,1:T(4,128)}), f32[1,2048,4,128]{3,2,0,1:T(4,128)}, u32[]{:S(2)}, u32[]{:S(2)}) %all-to-all-start) | async-done | bytes 4194336 | tf_op jit(solution)/shard_map/all_to_all | solution.py:68
  327.5 5.3 copy.41
  332.9 5.1 multiply_reduce_fusion.1
  344.1 155.1 %all-reduce.2.cloned.1.call-done = bf16[512,4096]{1,0:T(8,128)(2,1)} async-done(((bf16[512,4096]{1,0:T(8,128)(2,1)}), bf16[512,4096]{1,0:T(8,128)(2,1)}) %all-reduce.2.cloned.1.call-update) | async-done | bytes 4194320 | tf_op jit(solution)/shard_map/psum | solution.py:80
  499.2 9.2 %convert_add_fusion = (f32[512,4096]{1,0:T(8,128)}, f32[512]{0:T(512)S(1)}) fusion(bf16[512,4096]{1,0:T(8,128)(2,1)} %all-gather.5.cloned.1.call-done, bf16[512,4096]{1,0:T(8,128)(2,1)} %all-reduce.2.cloned.1.call-done), kind=kLoop, calls=%fused_computation.14 | loop fusion | flops 10485248 | bytes 16779264 | tf_op jit(solution)/shard_map/add | solution.py:83
  508.4 131.6 %all-gather.9.cloned.1.call-done = bf16[4096,2,1376]{0,2,1:T(8,128)(2,1)} async-done(((bf16[1024,2,1376]{0,2,1:T(8,128)(2,1)}), bf16[4096,2,1376]{0,2,1:T(8,128)(2,1)}) %all-gather.9.cloned.1.call-update) | async-done | bytes 22544400 | tf_op jit(solution)/shard_map/all_gather | solution.py:89
  639.9 20.5 %fusion.16 = f32[512,2,1376]{0,2,1:T(8,128)} fusion(bf16[4096,2,1376]{0,2,1:T(8,128)(2,1)} %all-gather.9.cloned.1.call-done, f32[4096]{0:T(1024)S(1)} %copy-done.6, f32[512]{0:T(512)S(1)} %add_rsqrt_fusion, bf16[512,4096]{1,0:T(8,128)(2,1)} %all-gather.5.cloned.1.call-done, bf16[512,4096]{1,0:T(8,128)(2,1)} %all-reduce.2.cloned.1.call-done), kind=kOutput, calls=%fused_computation.25 | convolution fusion | flops 11555307520 | bytes 36587520 | tf_op jit(solution)/shard_map/td,dgf->tgf/dot_general | solution.py:86
  660.4 55.6 %all-gather.11.cloned.1.call-done = bf16[1376,4096]{1,0:T(8,128)(2,1)} async-done(((bf16[1376,1024]{1,0:T(8,128)(2,1)}), bf16[1376,4096]{1,0:T(8,128)(2,1)}) %all-gather.11.cloned.1.call-update) | async-done | bytes 11272208 | tf_op jit(solution)/shard_map/all_gather | solution.py:95
  716.0 13.6 %convolution_convert_fusion = bf16[512,4096]{1,0:T(8,128)(2,1)} fusion(bf16[1376,4096]{1,0:T(8,128)(2,1)} %all-gather.11.cloned.1.call-done, f32[512,2,1376]{0,2,1:T(8,128)} %fusion.16), kind=kOutput, calls=%fused_computation.22 | convolution fusion | flops 5777686528 | bytes 21102592 | tf_op jit(solution)/shard_map/dot_general | solution.py:93
  729.6 88.4 %reduce-scatter.2.cloned.1.call-done = bf16[64,4096]{1,0:T(8,128)(2,1)} async-done(((bf16[512,4096]{1,0:T(8,128)(2,1)}), bf16[64,4096]{1,0:T(8,128)(2,1)}) %reduce-scatter.2.cloned.1.call-update) | async-done | bytes 524304 | tf_op jit(solution)/shard_map/reduce_scatter | solution.py:98
  (67 shorter events, 50.1 us)
Async XLA Ops:
  6.5 78.5 %all-gather.5.cloned.1.call-start = ((), (), s32[]{:S(2)}) async-start(), calls=%async_computation.4 | async-start | bytes 4718592 | tf_op jit(solution)/shard_map/all_gather | solution.py:23
  7.3 114.9 %all-gather.7.cloned.1.call-start = ((), (), s32[]{:S(2)}) async-start(), calls=%async_computation.5 | async-start | bytes 2621440 | tf_op jit(solution)/shard_map/all_gather | solution.py:31
  7.3 80.8 %copy-start.5 = (f32[4096]{0:T(1024)S(1)}, f32[4096]{0:T(1024)}, u32[]{:S(2)}) copy-start(f32[4096]{0:T(1024)} %param.10) | copy-start | bytes 49156
  107.4 7.1 copy-start.4
  141.8 19.2 %copy-start.2 = (bf16[1,2048,4,128]{1,3,2,0:T(8,128)(2,1)S(1)}, bf16[1,2048,4,128]{1,3,2,0:T(8,128)(2,1)}, u32[]{:S(2)}) copy-start(bf16[1,2048,4,128]{1,3,2,0:T(8,128)(2,1)} %copy.49) | copy-start | bytes 6291460
  141.8 19.2 %copy-start.3 = (bf16[512,4,128]{0,2,1:T(8,128)(2,1)S(1)}, bf16[512,4,128]{0,2,1:T(8,128)(2,1)}, u32[]{:S(2)}) copy-start(bf16[512,4,128]{0,2,1:T(8,128)(2,1)} %copy.45) | copy-start | bytes 1572868
  198.0 19.2 %copy-start.1 = (bf16[1,2048,4,128]{1,3,2,0:T(8,128)(2,1)S(1)}, bf16[1,2048,4,128]{1,3,2,0:T(8,128)(2,1)}, u32[]{:S(2)}) copy-start(bf16[1,2048,4,128]{1,3,2,0:T(8,128)(2,1)} %copy.44) | copy-start | bytes 6291460
  247.0 14.4 %all-to-all-start.1 = ((f32[4,1,2048]{2,1,0:T(1,128)}), f32[4,1,2048]{2,1,0:T(1,128)S(1)}, u32[]{:S(2)}, u32[]{:S(2)}) async-start(f32[4,1,2048]{2,1,0:T(1,128)} %reshape.59), calls=%async_computation.1 | async-start | bytes 65536 | tf_op jit(solution)/shard_map/all_to_all | solution.py:66
  261.3 13.2 %all-to-all-start.2 = ((f32[4,1,2048]{2,1,0:T(1,128)}), f32[4,1,2048]{2,1,0:T(1,128)S(1)}, u32[]{:S(2)}, u32[]{:S(2)}) async-start(f32[4,1,2048]{2,1,0:T(1,128)} %reshape.61), calls=%async_computation.2 | async-start | bytes 65536 | tf_op jit(solution)/shard_map/all_to_all | solution.py:67
  274.5 53.1 %all-to-all-start = ((f32[1,2048,4,128]{3,2,0,1:T(4,128)}), f32[1,2048,4,128]{3,2,0,1:T(4,128)}, u32[]{:S(2)}, u32[]{:S(2)}) async-start(f32[1,2048,4,128]{3,2,0,1:T(4,128)} %copy.37), calls=%async_computation | async-start | bytes 8388608 | tf_op jit(solution)/shard_map/all_to_all | solution.py:68
  279.3 219.8 %all-reduce.2.cloned.1.call-start = ((), (), s32[]{:S(2)}) async-start(), calls=%async_computation.6 | async-start | bytes 8388608 | tf_op jit(solution)/shard_map/psum | solution.py:80
  332.9 5.3 copy-start
  342.7 297.3 %all-gather.9.cloned.1.call-start = ((), (), s32[]{:S(2)}) async-start(), calls=%async_computation.7 | async-start | bytes 28180480 | tf_op jit(solution)/shard_map/all_gather | solution.py:89
  343.2 372.8 %all-gather.11.cloned.1.call-start = ((), (), s32[]{:S(2)}) async-start(), calls=%async_computation.8 | async-start | bytes 14090240 | tf_op jit(solution)/shard_map/all_gather | solution.py:95
  343.8 296.1 %copy-start.6 = (f32[4096]{0:T(1024)S(1)}, f32[4096]{0:T(1024)}, u32[]{:S(2)}) copy-start(f32[4096]{0:T(1024)} %param.15) | copy-start | bytes 49156
  343.8 474.2 %reduce-scatter.2.cloned.1.call-start = ((), (), s32[]{:S(2)}) async-start(), calls=%async_computation.9 | async-start | bytes 4718592 | tf_op jit(solution)/shard_map/reduce_scatter | solution.py:98
Sparse Core Ops, SparseCore 0:
  9.5 75.5 all-gather.4
  101.0 21.0 all-gather.6
  342.8 156.3 all-reduce.1
  500.6 139.2 all-gather.8
  641.3 74.6 all-gather.10
  729.7 88.2 reduce-scatter.1
where the time goes:
time: 835 us; the launch traced here: 827 us
  waiting for transfers between devices  540 us (65%)
  matrix products  124 us (15%)
  other arithmetic  84.6 us (10%)
  local copies, waits for them, and re-layouts  52.2 us (6%)
  between operations  13.9 us (2%)
  starting transfers between devices  12.2 us (1%)
    psum x1, waiting for transfers between devices, per_device(): lax.psum(jnp.dot(attended, w_out, preferred_element_type=jnp.float32).ast...  155 us
    all_gather x1, waiting for transfers between devices, per_device(): lax.all_gather(w_gate_up, 'kv', axis=0, tiled=True)  132 us
    reduce_scatter x1, waiting for transfers between devices, per_device(): lax.psum_scatter(down_terms.astype(jnp.bfloat16), 'tp', scatter_dimension...  88.4 us
    all_gather x1, waiting for transfers between devices, per_device(): block_input = lax.all_gather(hidden_in, 'tp', axis=0, tiled=True)  65.3 us
    all_gather x1, waiting for transfers between devices, per_device(): lax.all_gather(w_down, 'kv', axis=1, tiled=True)  55.6 us
    all_to_all x1, waiting for transfers between devices, per_device(): lax.all_to_all(accum_all[None], 'kv', split_axis=1, concat_axis=0, tiled=...  42 us
    dot_general x2, matrix products, per_device(): jnp.einsum('qhd,khd->hqk', query_block, joined_key_rows, preferred_elemen...  38.7 us
    reduce_sum x2, other arithmetic, per_device(): masses.append(jnp.sum(raw_weights, axis=2).T)  38.4 us
  transfers between devices with their start and end apart: 9, of which 7 were waited for; matrix products, arithmetic and copies ran while one was open for 11% of the time, Pallas kernels for 0%

commit v1 on v0

--- a/solution.py
+++ b/solution.py
@@ -6,6 +6,22 @@
 
 EPSILON = 1e-05
 MASKED = -1e30
+
+
+def product_in_turn(x, axis, dim, contribution):
+    size, index, extent = (lax.axis_size(axis), lax.axis_index(axis), x.shape[dim])
+    right = [(i, (i + 1) % size) for i in range(size)]
+    left = [(i, (i - 1) % size) for i in range(size)]
+    half = size // 2
+    from_left = from_right = x
+    total = contribution(x, index * extent)
+    for step in range(1, half + 1):
+        from_left = lax.ppermute(from_left, axis, right)
+        if step < size - half:
+            from_right = lax.ppermute(from_right, axis, left)
+            total = total + contribution(from_right, (index + step) % size * extent)
+        total = total + contribution(from_left, (index - step) % size * extent)
+    return total
 
 
 def rms_scale(values_in, gain_vector):
@@ -83,11 +99,16 @@
     residual = block_input.astype(jnp.float32) + heads_sum
     mlp_in = rms_scale(residual, gain_mlp)
     residual_own = lax.dynamic_slice_in_dim(residual, tp_index * own_rows, own_rows, 0)
-    gate_up = jnp.einsum(
-        "td,dgf->tgf",
-        mlp_in,
-        lax.all_gather(w_gate_up, "kv", axis=0, tiled=True),
-        preferred_element_type=jnp.float32,
+    gate_up = product_in_turn(
+        w_gate_up,
+        "kv",
+        0,
+        lambda own_block, offset: jnp.einsum(
+            "td,dgf->tgf",
+            lax.dynamic_slice_in_dim(mlp_in, offset, own_block.shape[0], axis=1),
+            own_block,
+            preferred_element_type=jnp.float32,
+        ),
     )
     activated = (jax.nn.silu(gate_up[:, 0, :]) * gate_up[:, 1, :]).astype(jnp.bfloat16)
     down_terms = jnp.dot(

time: 835 us -> 712 us (0.85)
  waiting for transfers between devices: 540 us -> 406 us
    ppermute x0 -> x3, waiting for transfers between devices: none -> 159 us  [the longest x2 159 us: product_in_turn(): from_left = lax.ppermute(from_left, axis, right)]
    all_gather x1 -> x0, waiting for transfers between devices: 132 us -> none  [per_device(): lax.all_gather(w_gate_up, 'kv', axis=0, tiled=True)]
    psum x1, waiting for transfers between devices: 155 us -> 32.5 us  [per_device(): lax.psum(jnp.dot(attended, w_out, preferred_element_type=jnp.float32).ast...]
    all_gather x1, waiting for transfers between devices: 55.6 us -> 16.4 us  [per_device(): lax.all_gather(w_down, 'kv', axis=1, tiled=True)]
    dot_general x1 -> x4, matrix products: 20.5 us -> 28.6 us  [per_device(): jnp.einsum('td,dgf->tgf', lax.dynamic_slice_in_dim(mlp_in, offset, own_bl...]
    unnamed x25 -> x29, local copies, waits for them, and re-layouts: 28.1 us -> 28.1 us
  transfers between devices with their start and end apart: 9 -> 11, of which waited for: 7 -> 8; matrix products, arithmetic and copies ran while one was open for 11% -> 14% of each run, Pallas kernels for 0% -> 0%
where the time goes in v1:
time: 712 us; the launch traced here: 704 us
  waiting for transfers between devices  406 us (57%)
  matrix products  132 us (19%)
  other arithmetic  86.9 us (12%)
  local copies, waits for them, and re-layouts  52.3 us (7%)
  between operations  13.7 us (2%)
  starting transfers between devices  13.5 us (2%)
    ppermute x2, waiting for transfers between devices, product_in_turn(): from_left = lax.ppermute(from_left, axis, right)  159 us
    reduce_scatter x1, waiting for transfers between devices, per_device(): lax.psum_scatter(down_terms.astype(jnp.bfloat16), 'tp', scatter_dimension...  88.9 us
    all_gather x1, waiting for transfers between devices, per_device(): block_input = lax.all_gather(hidden_in, 'tp', axis=0, tiled=True)  65.3 us
    all_to_all x1, waiting for transfers between devices, per_device(): lax.all_to_all(accum_all[None], 'kv', split_axis=1, concat_axis=0, tiled=...  42.3 us
    reduce_sum x2, other arithmetic, per_device(): masses.append(jnp.sum(raw_weights, axis=2).T)  38.4 us
    dot_general x2, matrix products, per_device(): jnp.einsum('qhd,khd->hqk', query_block, joined_key_rows, preferred_elemen...  38.4 us
    dot_general x2, matrix products, per_device(): jnp.einsum('hqk,khd->qhd', raw_weights.astype(jnp.bfloat16), joined_value...  35.8 us
    psum x1, waiting for transfers between devices, per_device(): lax.psum(jnp.dot(attended, w_out, preferred_element_type=jnp.float32).ast...  32.5 us
  transfers between devices with their start and end apart: 11, of which 8 were waited for; matrix products, arithmetic and copies ran while one was open for 14% of the time, Pallas kernels for 0%

profile of v1, /device:TPU:0, one launch (start us, length us, event | category | flops | bytes accessed | tf_op | source)
XLA Modules:
  0.0 704.0 jit_solution(4152850163955019507)
XLA Ops:
  7.3 12.4 %copy.51 = bf16[512,8,4,384]{3,1,2,0:T(8,128)(2,1)} copy(bf16[512,8,4,384]{3,2,1,0:T(4,128)(2,1)} %bitcast.62) | data formatting | bytes 25165824
  19.7 65.3 %all-gather.4.cloned.1.call-done = bf16[512,4096]{1,0:T(8,128)(2,1)} async-done(((bf16[64,4096]{1,0:T(8,128)(2,1)}), bf16[512,4096]{1,0:T(8,128)(2,1)}) %all-gather.4.cloned.1.call-update) | async-done | bytes 4194320 | tf_op jit(solution)/shard_map/all_gather | solution.py:39
  88.1 11.0 %fusion.19 = bf16[512,1536]{1,0:T(8,128)(2,1)S(1)} fusion(bf16[4096,1536]{1,0:T(8,128)(2,1)} %bitcast.63, bf16[512,4096]{1,0:T(8,128)(2,1)} %all-gather.4.cloned.1.call-done, f32[4096]{0:T(1024)S(1)} %copy-done.8, f32[512]{0:T(512)S(1)} %add_rsqrt_fusion.1), kind=kOutput, calls=%fused_computation.34 | convolution fusion | flops 6451625984 | bytes 18368512 | tf_op jit(solution)/shard_map/dot_general | solution.py:43
  100.9 6.4 fusion.71
  122.2 19.3 %fusion.1 = (f32[4,1024]{1,0:T(4,128)S(1)}, f32[4,1024,2560]{2,1,0:T(8,128)}) fusion(pred[2560]{0:T(1024)(128)(4,1)S(1)} %pad_add_fusion.1, bf16[512,4,128]{2,0,1:T(8,128)(2,1)S(1)} %copy.48, bf16[2048,4,128]{2,0,1:T(8,128)(2,1)} %get-tuple-element.26, bf16[2048,4,128]{2,0,1:T(8,128)(2,1)} %all-gather.6.cloned.1.call-done), kind=kOutput, calls=%fused_computation.5 | convolution fusion | flops 2721050624 | bytes 45632000 | tf_op jit(solution)/shard_map/qhd,khd->hqk/dot_general | solution.py:60
  141.5 19.2 %fusion.4 = f32[4,1024]{1,0:T(4,128)S(1)} fusion(f32[4,1024,2560]{2,1,0:T(8,128)} %get-tuple-element.19, f32[4,1024]{1,0:T(4,128)S(1)} %get-tuple-element.18, pred[2560]{0:T(1024)(128)(4,1)S(1)} %pad_add_fusion.1), kind=kLoop, calls=%fused_computation.8 | loop fusion | flops 52424704 | bytes 41978368 | tf_op jit(solution)/shard_map/reduce_sum | solution.py:69
  160.7 17.9 %fusion.33 = f32[1024,4,128]{0,2,1:T(8,128)} fusion(f32[4,1024,2560]{2,1,0:T(8,128)} %get-tuple-element.19, f32[4,1024]{1,0:T(4,128)S(1)} %get-tuple-element.18, pred[2560]{0:T(1024)(128)(4,1)S(1)} %pad_add_fusion.1, bf16[512,4,128]{0,2,1:T(8,128)(2,1)S(1)} %copy-done.5, bf16[2048,4,128]{0,2,1:T(8,128)(2,1)S(1)} %bitcast.71), kind=kOutput, calls=%fused_computation.48 | convolution fusion | flops 2742026240 | bytes 46680576 | tf_op jit(solution)/shard_map/hqk,khd->qhd/dot_general | solution.py:71
  178.6 19.1 %fusion = (f32[4,1024]{1,0:T(4,128)S(1)}, f32[4,1024,2560]{2,1,0:T(8,128)}) fusion(pred[2560]{0:T(1024)(128)(4,1)S(1)} %pad_add_fusion, bf16[512,4,128]{2,0,1:T(8,128)(2,1)S(1)} %copy.48, bf16[2048,4,128]{2,0,1:T(8,128)(2,1)S(1)} %get-tuple-element.27, bf16[2048,4,128]{2,0,1:T(8,128)(2,1)} %all-gather.6.cloned.1.call-done), kind=kOutput, calls=%fused_computation.4 | convolution fusion | flops 2721050624 | bytes 45632000 | tf_op jit(solution)/shard_map/qhd,khd->hqk/dot_general | solution.py:60
  197.7 19.2 %fusion.2 = f32[4,1024]{1,0:T(4,128)S(1)} fusion(f32[4,1024,2560]{2,1,0:T(8,128)} %get-tuple-element.21, f32[4,1024]{1,0:T(4,128)S(1)} %get-tuple-element.20, pred[2560]{0:T(1024)(128)(4,1)S(1)} %pad_add_fusion), kind=kLoop, calls=%fused_computation.6 | loop fusion | flops 52424704 | bytes 41978368 | tf_op jit(solution)/shard_map/reduce_sum | solution.py:69
  216.9 17.9 %fusion.30 = f32[1024,4,128]{0,2,1:T(8,128)} fusion(f32[4,1024,2560]{2,1,0:T(8,128)} %get-tuple-element.21, f32[4,1024]{1,0:T(4,128)S(1)} %get-tuple-element.20, pred[2560]{0:T(1024)(128)(4,1)S(1)} %pad_add_fusion, bf16[512,4,128]{0,2,1:T(8,128)(2,1)S(1)} %copy-done.5, bf16[2048,4,128]{0,2,1:T(8,128)(2,1)S(1)} %bitcast.70), kind=kOutput, calls=%fused_computation.47 | convolution fusion | flops 2742026240 | bytes 46680576 | tf_op jit(solution)/shard_map/hqk,khd->qhd/dot_general | solution.py:71
  235.7 9.7 %reduce.2 = f32[2048,4]{1,0:T(8,128)S(1)} reduce(f32[2048,1,4]{2,1,0:T(1,128)S(1)} %bitcast.66, f32[]{:T(128)} %broadcast.101), dimensions={1}, to_apply=%bitcast.50.reduce_sub_computation | reduce | bytes 65540
  250.5 9.3 %reduce = f32[2048,4]{1,0:T(8,128)S(1)} reduce(f32[2048,1,4]{2,1,0:T(1,128)S(1)} %bitcast.67, f32[]{:T(128)} %broadcast.101), dimensions={1}, to_apply=%bitcast.52.reduce_sub_computation | reduce | bytes 65540
  285.1 42.3 %all-to-all-done = f32[1,2048,4,128]{3,2,0,1:T(4,128)} async-done(((f32[1,2048,4,128]{3,2,0,1:T(4,128)}), f32[1,2048,4,128]{3,2,0,1:T(4,128)}, u32[]{:S(2)}, u32[]{:S(2)}) %all-to-all-start) | async-done | bytes 4194336 | tf_op jit(solution)/shard_map/all_to_all | solution.py:84
  327.4 5.3 copy.41
  344.9 121.6 %collective-permute-done.1 = bf16[1024,2,1376]{0,2,1:T(8,128)(2,1)} collective-permute-done((bf16[1024,2,1376]{0,2,1:T(8,128)(2,1)}, bf16[1024,2,1376]{0,2,1:T(8,128)(2,1)}, u32[]{:S(2)}, u32[]{:S(2)}) %collective-permute-start.1) | collective-permute-done | bytes 5636128 | tf_op jit(solution)/shard_map/ppermute | solution.py:19
  466.5 32.5 %all-reduce.2.cloned.1.call-done = bf16[512,4096]{1,0:T(8,128)(2,1)} async-done(((bf16[512,4096]{1,0:T(8,128)(2,1)}), bf16[512,4096]{1,0:T(8,128)(2,1)}) %all-reduce.2.cloned.1.call-update) | async-done | bytes 4194320 | tf_op jit(solution)/shard_map/psum | solution.py:96
  499.0 8.9 %convert_add_fusion = (f32[512,4096]{1,0:T(8,128)}, f32[512]{0:T(512)S(1)}) fusion(bf16[512,4096]{1,0:T(8,128)(2,1)} %all-gather.4.cloned.1.call-done, bf16[512,4096]{1,0:T(8,128)(2,1)} %all-reduce.2.cloned.1.call-done), kind=kLoop, calls=%fused_computation.14 | loop fusion | flops 10485248 | bytes 16779264 | tf_op jit(solution)/shard_map/add | solution.py:99
  510.4 6.3 fusion.45
  522.0 7.7 %fusion.43 = f32[512,2,1376]{0,2,1:T(8,128)} fusion(bf16[1024,2,1376]{0,2,1:T(8,128)(2,1)} %collective-permute-done, bf16[512,4096]{1,0:T(8,128)(2,1)S(1)} %multiply_convert_fusion, s32[]{:T(128)S(6)} %select_n.56), kind=kOutput, calls=%fused_computation.55 | convolution fusion | flops 2885681152 | bytes 12320772 | tf_op jit(solution)/shard_map/td,dgf->tgf/dot_general | solution.py:106
  529.7 37.0 %collective-permute-done.2 = bf16[1024,2,1376]{0,2,1:T(8,128)(2,1)} collective-permute-done((bf16[1024,2,1376]{0,2,1:T(8,128)(2,1)}, bf16[1024,2,1376]{0,2,1:T(8,128)(2,1)}, u32[]{:S(2)}, u32[]{:S(2)}) %collective-permute-start.2) | collective-permute-done | bytes 5636128 | tf_op jit(solution)/shard_map/ppermute | solution.py:19
  566.7 9.4 %add_add_fusion = f32[512,2,1376]{0,2,1:T(8,128)} fusion(f32[512,2,1376]{0,2,1:T(8,128)S(1)} %fusion.41, f32[512,2,1376]{0,2,1:T(8,128)S(1)} %fusion.45, f32[512,2,1376]{0,2,1:T(8,128)} %fusion.43, bf16[1024,2,1376]{0,2,1:T(8,128)(2,1)} %collective-permute-done.2, bf16[512,4096]{1,0:T(8,128)(2,1)S(1)} %multiply_convert_fusion, s32[]{:T(128)S(6)} %select_n.60), kind=kOutput, calls=%fused_computation.24 | convolution fusion | flops 2889908224 | bytes 29229060 | tf_op jit(solution)/shard_map/td,dgf->tgf/dot_general | solution.py:106
  576.1 16.4 %all-gather.8.cloned.1.call-done = bf16[1376,4096]{1,0:T(8,128)(2,1)} async-done(((bf16[1376,1024]{1,0:T(8,128)(2,1)}), bf16[1376,4096]{1,0:T(8,128)(2,1)}) %all-gather.8.cloned.1.call-update) | async-done | bytes 11272208 | tf_op jit(solution)/shard_map/all_gather | solution.py:116
  592.4 13.7 %convolution_convert_fusion = bf16[512,4096]{1,0:T(8,128)(2,1)} fusion(bf16[1376,4096]{1,0:T(8,128)(2,1)} %all-gather.8.cloned.1.call-done, f32[512,2,1376]{0,2,1:T(8,128)} %add_add_fusion), kind=kOutput, calls=%fused_computation.22 | convolution fusion | flops 5777686528 | bytes 21102592 | tf_op jit(solution)/shard_map/dot_general | solution.py:114
  606.1 88.9 %reduce-scatter.2.cloned.1.call-done = bf16[64,4096]{1,0:T(8,128)(2,1)} async-done(((bf16[512,4096]{1,0:T(8,128)(2,1)}), bf16[64,4096]{1,0:T(8,128)(2,1)}) %reduce-scatter.2.cloned.1.call-update) | async-done | bytes 524304 | tf_op jit(solution)/shard_map/reduce_scatter | solution.py:119
  (78 shorter events, 73.7 us)
Async XLA Ops:
  6.5 78.5 %all-gather.4.cloned.1.call-start = ((), (), s32[]{:S(2)}) async-start(), calls=%async_computation.4 | async-start | bytes 4718592 | tf_op jit(solution)/shard_map/all_gather | solution.py:39
  7.3 114.9 %all-gather.6.cloned.1.call-start = ((), (), s32[]{:S(2)}) async-start(), calls=%async_computation.5 | async-start | bytes 2621440 | tf_op jit(solution)/shard_map/all_gather | solution.py:47
  7.3 80.8 %copy-start.8 = (f32[4096]{0:T(1024)S(1)}, f32[4096]{0:T(1024)}, u32[]{:S(2)}) copy-start(f32[4096]{0:T(1024)} %param.10) | copy-start | bytes 49156
  107.4 7.1 %copy-start.7 = (s32[2]{0:T(128)S(1)}, s32[2]{0:T(128)}, u32[]{:S(2)}) copy-start(s32[2]{0:T(128)} %param.13) | copy-start | bytes 28
  141.5 19.2 %copy-start.4 = (bf16[1,2048,4,128]{1,3,2,0:T(8,128)(2,1)S(1)}, bf16[1,2048,4,128]{1,3,2,0:T(8,128)(2,1)}, u32[]{:S(2)}) copy-start(bf16[1,2048,4,128]{1,3,2,0:T(8,128)(2,1)} %copy.49) | copy-start | bytes 6291460
  141.5 19.2 %copy-start.5 = (bf16[512,4,128]{0,2,1:T(8,128)(2,1)S(1)}, bf16[512,4,128]{0,2,1:T(8,128)(2,1)}, u32[]{:S(2)}) copy-start(bf16[512,4,128]{0,2,1:T(8,128)(2,1)} %copy.45) | copy-start | bytes 1572868
  197.7 19.2 %copy-start.3 = (bf16[1,2048,4,128]{1,3,2,0:T(8,128)(2,1)S(1)}, bf16[1,2048,4,128]{1,3,2,0:T(8,128)(2,1)}, u32[]{:S(2)}) copy-start(bf16[1,2048,4,128]{1,3,2,0:T(8,128)(2,1)} %copy.44) | copy-start | bytes 6291460
  246.8 14.3 %all-to-all-start.1 = ((f32[4,1,2048]{2,1,0:T(1,128)}), f32[4,1,2048]{2,1,0:T(1,128)S(1)}, u32[]{:S(2)}, u32[]{:S(2)}) async-start(f32[4,1,2048]{2,1,0:T(1,128)} %reshape.62), calls=%async_computation.1 | async-start | bytes 65536 | tf_op jit(solution)/shard_map/all_to_all | solution.py:82
  261.2 13.2 %all-to-all-start.2 = ((f32[4,1,2048]{2,1,0:T(1,128)}), f32[4,1,2048]{2,1,0:T(1,128)S(1)}, u32[]{:S(2)}, u32[]{:S(2)}) async-start(f32[4,1,2048]{2,1,0:T(1,128)} %reshape.64), calls=%async_computation.2 | async-start | bytes 65536 | tf_op jit(solution)/shard_map/all_to_all | solution.py:83
  274.3 53.1 %all-to-all-start = ((f32[1,2048,4,128]{3,2,0,1:T(4,128)}), f32[1,2048,4,128]{3,2,0,1:T(4,128)}, u32[]{:S(2)}, u32[]{:S(2)}) async-start(f32[1,2048,4,128]{3,2,0,1:T(4,128)} %copy.37), calls=%async_computation | async-start | bytes 8388608 | tf_op jit(solution)/shard_map/all_to_all | solution.py:84
  279.2 219.9 %all-reduce.2.cloned.1.call-start = ((), (), s32[]{:S(2)}) async-start(), calls=%async_computation.6 | async-start | bytes 8388608 | tf_op jit(solution)/shard_map/psum | solution.py:96
  332.7 5.3 copy-start.2
  342.5 249.9 %all-gather.8.cloned.1.call-start = ((), (), s32[]{:S(2)}) async-start(), calls=%async_computation.7 | async-start | bytes 14090240 | tf_op jit(solution)/shard_map/all_gather | solution.py:116
  343.1 351.9 %reduce-scatter.2.cloned.1.call-start = ((), (), s32[]{:S(2)}) async-start(), calls=%async_computation.8 | async-start | bytes 4718592 | tf_op jit(solution)/shard_map/reduce_scatter | solution.py:119
  343.1 123.4 %collective-permute-start.1 = (bf16[1024,2,1376]{0,2,1:T(8,128)(2,1)}, bf16[1024,2,1376]{0,2,1:T(8,128)(2,1)}, u32[]{:S(2)}, u32[]{:S(2)}) collective-permute-start(bf16[1024,2,1376]{0,2,1:T(8,128)(2,1)} %param.16), channel_id=1, source_target_pairs={{0,1},{1,2},{2,3},{3,0},{4,5},{5,6},{6,7},{7,4},{8,9},{9,10},{10,1... | collective-permute-start | bytes 16908296 | tf_op jit(solution)/shard_map/ppermute | solution.py:19
  343.2 178.8 %collective-permute-start = (bf16[1024,2,1376]{0,2,1:T(8,128)(2,1)}, bf16[1024,2,1376]{0,2,1:T(8,128)(2,1)}, u32[]{:S(2)}, u32[]{:S(2)}) collective-permute-start(bf16[1024,2,1376]{0,2,1:T(8,128)(2,1)} %param.16), channel_id=1, source_target_pairs={{0,3},{1,0},{2,1},{3,2},{4,7},{5,4},{6,5},{7,6},{8,11},{9,8},{10,9... | collective-permute-start | bytes 16908296 | tf_op jit(solution)/shard_map/ppermute | solution.py:21
  466.5 100.2 %collective-permute-start.2 = (bf16[1024,2,1376]{0,2,1:T(8,128)(2,1)}, bf16[1024,2,1376]{0,2,1:T(8,128)(2,1)}, u32[]{:S(2)}, u32[]{:S(2)}) collective-permute-start(bf16[1024,2,1376]{0,2,1:T(8,128)(2,1)} %collective-permute-done.1), channel_id=1, source_target_pairs={{0,1},{1,2},{2,3},{3,0},{4,5},{5,6},{6,7},{7,4},{8,9},{9,10},{10,1... | collective-permute-start | bytes 16908296 | tf_op jit(solution)/shard_map/ppermute | solution.py:19
  466.5 41.5 %copy-start.6 = (f32[4096]{0:T(1024)S(1)}, f32[4096]{0:T(1024)}, u32[]{:S(2)}) copy-start(f32[4096]{0:T(1024)} %param.15) | copy-start | bytes 49156
  499.0 9.0 %copy-start = (bf16[512,4096]{1,0:T(8,128)(2,1)S(1)}, bf16[512,4096]{1,0:T(8,128)(2,1)}, u32[]{:S(2)}) copy-start(bf16[512,4096]{1,0:T(8,128)(2,1)} %all-gather.4.cloned.1.call-done) | copy-start | bytes 12582916
  499.0 9.0 %copy-start.1 = (bf16[512,4096]{1,0:T(8,128)(2,1)S(1)}, bf16[512,4096]{1,0:T(8,128)(2,1)}, u32[]{:S(2)}) copy-start(bf16[512,4096]{1,0:T(8,128)(2,1)} %all-reduce.2.cloned.1.call-done) | copy-start | bytes 12582916
Sparse Core Ops, SparseCore 0:
  9.5 75.5 all-gather.3
  101.0 21.0 all-gather.5
  342.6 156.3 all-reduce.1
  500.5 91.9 all-gather.7
  606.2 88.7 reduce-scatter.1
